TPU v7x, 128 devices: a whole 4x4x4 slice. The times are simulated.
128 devices in a mesh: dp: 64 (over y, z_lo, x, core), rep: 2 (over z_hi).
Axes of the slice: x: 4, y: 4, z: 4 (z_hi: 2, z_lo: 2; z = z_hi * 2 + z_lo), core: 2. Of those that a mesh axis runs over, the one named last changes fastest.
Arguments:
- queries: bfloat16 [8192, 2048], P(('dp', 'rep')), may hold values from -24 to 24
- documents: bfloat16 [8192, 2048], P(('dp', 'rep')), may hold values from -24 to 24
- partner: int32 [8192], P(('dp', 'rep')), may hold values from 0 to 8191, each once
Outputs:
- grad_queries: float32 [8192, 2048], P(('dp', 'rep'))
- grad_documents: float32 [8192, 2048], P(('dp', 'rep'))
Inputs may be any that keep to these rules, and one draw needn't show every extreme that they name: `partner`: every document index appears exactly once.
All inputs are finite; a program needn't handle non-finite values.
Results may differ from a plain program's by a relative error of at most 0.0031.
Values may be sent and summed in bfloat16 or wider, within the bound.
A program may use at most 256 MiB of HBM per device.

v0:
```python
import jax
import jax.numpy as jnp
from jax import lax
from jax.sharding import Mesh
from jax.sharding import PartitionSpec as P

WIDTHS = 9
DP = ("dp_0", "dp_1", "dp_2", "dp_3")
DP_REP = ("dp_0", "dp_1", "dp_2", "dp_3", "rep")
logit_gain = 3.0


def laid_out(blocks, dim):
    blocks = jnp.moveaxis(blocks, 0, dim)
    shape = blocks.shape
    return blocks.reshape(*shape[:dim], shape[dim] * shape[dim + 1], *shape[dim + 2 :])


def copy_for_each(x, axis):
    copies = jnp.broadcast_to(x, (lax.axis_size(axis), *x.shape))
    return lax.all_to_all(copies, axis, split_axis=0, concat_axis=0, tiled=True)


def collect(x, axis, dim):
    return laid_out(copy_for_each(x, axis), dim)


def collected_together(x, axis):
    leaves = jax.tree.leaves(x)
    turns = sorted(range(len(leaves)), key=lambda k: -leaves[k].size)
    width = (1, *leaves[turns[0]].shape)[-1]
    lines = [
        jnp.pad(leaves[k].reshape(-1), (0, -leaves[k].size % width)).reshape(-1, width)
        for k in turns
    ]
    both, at, found = (copy_for_each(jnp.concatenate(lines), axis), 0, {})
    for k, line in zip(turns, lines):
        piece = both[:, at : at + len(line)].reshape(len(both), -1)
        found[k] = piece[:, : leaves[k].size].reshape(-1, *leaves[k].shape)
        at += len(line)
    numbers = iter(range(len(leaves)))
    return jax.tree.map(lambda _: found[next(numbers)], x)


def folded_in_pairs(pieces, combine):
    while len(jax.tree.leaves(pieces)[0]) > 1:
        pieces = jax.vmap(combine)(
            *(jax.tree.map(lambda part: part[side::2], pieces) for side in (0, 1))
        )
    return jax.tree.map(lambda part: part[0], pieces)


def merged(x, axis, combine):
    pieces = collected_together(x, axis)
    return folded_in_pairs(pieces, combine)


def cut_along(x, dim, size):
    shape = x.shape
    blocks = x.reshape(*shape[:dim], size, shape[dim] // size, *shape[dim + 1 :])
    return jnp.moveaxis(blocks, dim, 0)


def sum_at_owner(x, axis, dim):
    blocks = cut_along(x, dim, lax.axis_size(axis))
    arrived = lax.all_to_all(blocks, axis, split_axis=0, concat_axis=0, tiled=True)
    return arrived.sum(axis=0)


def sum_by_chip(x, chips, core, dim):
    sizes = (lax.axis_size(chips), lax.axis_size(core))
    blocks = cut_along(x, dim, sizes[0] * sizes[1])
    inside = blocks.shape[1:]
    blocks = blocks.reshape(*sizes, *inside).swapaxes(0, 1).reshape(-1, *inside)
    blocks = lax.psum_scatter(blocks, core, scatter_dimension=0, tiled=True)
    return lax.psum_scatter(blocks, chips, scatter_dimension=0, tiled=True)[0]


def contract(first_op, second_op):
    return lax.dot_general(
        first_op, second_op, (((1,), (1,)), ((), ())), preferred_element_type=jnp.float32
    )


def width_list(feature_dim):
    return [feature_dim >> WIDTHS - 1 - nested for nested in range(WIDTHS)]


def scores(first_op, second_op):
    uppers = width_list(first_op.shape[1])
    result = []
    running = jnp.zeros((first_op.shape[0], second_op.shape[0]), jnp.float32)
    lower_col = 0
    for upper_col in uppers:
        running = running + contract(
            first_op[:, lower_col:upper_col], second_op[:, lower_col:upper_col]
        )
        result.append(running * (logit_gain * upper_col ** (-0.5)))
        lower_col = upper_col
    return result


def band_sums(logit_list, total_list, target, uppers):
    bands = [None] * len(uppers)
    running = None
    for nested in reversed(range(len(uppers))):
        scale = logit_gain * uppers[nested] ** (-0.5)
        weight = (jnp.exp(logit_list[nested] - total_list[nested]) - target) * scale
        running = weight if running is None else running + weight
        bands[nested] = running.astype(jnp.bfloat16)
    return bands


def spread(bands, operand, uppers, transposed):
    pieces = []
    lower_col = 0
    for nested, upper_col in enumerate(uppers):
        block_part = operand[:, lower_col:upper_col]
        if transposed:
            product = lax.dot_general(
                bands[nested],
                block_part,
                (((0,), (0,)), ((), ())),
                preferred_element_type=jnp.float32,
            )
        else:
            product = jnp.dot(bands[nested], block_part, preferred_element_type=jnp.float32)
        pieces.append(product)
        lower_col = upper_col
    return jnp.concatenate(pieces, axis=1)


def combine(first_pair, second_pair):
    biggest = jnp.maximum(first_pair[0], second_pair[0])
    return (
        biggest,
        first_pair[1] * jnp.exp(first_pair[0] - biggest)
        + second_pair[1] * jnp.exp(second_pair[0] - biggest),
    )


def on_device(queries, documents, partner):
    own_rows = queries.shape[0]
    uppers = width_list(queries.shape[1])
    rep_index = lax.axis_index("rep")
    rep_count = lax.axis_size("rep")
    pair_rows, pair_partner = (collect(queries, "rep", 0), collect(partner, "rep", 0))
    partner_docs = lax.all_gather(documents, DP, axis=0, tiled=True)
    col_pos = jnp.arange(partner_docs.shape[0], dtype=jnp.int32)
    col_ids = (col_pos // own_rows * rep_count + rep_index) * own_rows + col_pos % own_rows
    target = (pair_partner[:, None] == col_ids[None, :]).astype(jnp.float32)
    logit_list = scores(pair_rows, partner_docs)
    row_peaks = jnp.stack([jnp.max(logits, axis=1) for logits in logit_list])
    masses = jnp.stack(
        [
            jnp.sum(jnp.exp(logits - row_peaks[nested][:, None]), axis=1)
            for nested, logits in enumerate(logit_list)
        ]
    )
    row_peaks, masses = merged((row_peaks, masses), "rep", combine)
    totals = row_peaks + jnp.log(masses)
    bands = band_sums(
        logit_list, [totals[nested][:, None] for nested in range(len(uppers))], target, uppers
    )
    partial_queries = spread(bands, partner_docs, uppers, False)
    grad_queries = sum_at_owner(partial_queries, "rep", 0)
    sliced = [factor for factor in bands]
    grad_documents = sum_by_chip(
        spread(sliced, pair_rows, uppers, True), ("dp_0", "dp_1", "dp_2"), "dp_3", 0
    )
    return (grad_queries, grad_documents)


def solution(mesh):
    finer = Mesh(
        mesh.devices.reshape(4, 2, 4, 2, mesh.shape["rep"]), ("dp_0", "dp_1", "dp_2", "dp_3", "rep")
    )
    placed = (P(DP_REP, None), P(DP_REP, None), P(DP_REP))
    return jax.shard_map(
        on_device,
        mesh=finer,
        in_specs=placed,
        out_specs=(P(DP_REP, None), P(DP_REP, None)),
        check_vma=False,
    )
```

profile of v0, /device:TPU:0, one launch (start us, length us, event | category | flops | bytes accessed | tf_op | source)
XLA Modules:
  0.0 521.3 jit_solution(7170143682551162871)
XLA Ops:
  9.7 5.3 %all-to-all-start = ((bf16[2,64,2048]{2,1,0:T(8,128)(2,1)}), bf16[2,64,2048]{2,1,0:T(8,128)(2,1)S(1)}, u32[]{:S(2)}, u32[]{:S(2)}) async-start(bf16[2,64,2048]{2,1,0:T(8,128)(2,1)} %broadcast_in_dim.10), calls=%async_computation | async-start | bytes 1048576 | tf_op jit(solution)/shard_map/all_to_all | solution.py:21
  15.0 9.5 %all-to-all-done = bf16[2,64,2048]{2,1,0:T(8,128)(2,1)S(1)} async-done(((bf16[2,64,2048]{2,1,0:T(8,128)(2,1)}), bf16[2,64,2048]{2,1,0:T(8,128)(2,1)S(1)}, u32[]{:S(2)}, u32[]{:S(2)}) %all-to-all-start) | async-done | bytes 524320 | tf_op jit(solution)/shard_map/all_to_all | solution.py:21
  25.0 3.2 all-to-all-start.2
  28.2 105.5 %all-gather.2.cloned.1.call-done = bf16[4096,2048]{1,0:T(8,128)(2,1)} async-done(((bf16[64,2048]{1,0:T(8,128)(2,1)}), bf16[4096,2048]{1,0:T(8,128)(2,1)}) %all-gather.2.cloned.1.call-update) | async-done | bytes 16777232 | tf_op jit(solution)/shard_map/all_gather | solution.py:148
  136.0 2.1 multiply_reduce_fusion.6
  138.6 2.1 multiply_reduce_fusion.5
  141.2 2.1 multiply_reduce_fusion.4
  143.9 2.1 multiply_reduce_fusion.3
  146.5 2.0 multiply_reduce_fusion.2
  149.0 2.5 multiply_reduce_fusion.1
  152.0 4.1 multiply_reduce_fusion
  156.6 5.7 %fusion.110 = (f32[128]{0:T(128)S(1)}, f32[128,4096]{1,0:T(8,128)S(1)}) fusion(f32[128,4096]{1,0:T(8,128)S(1)} %get-tuple-element.34, bf16[4096,2048]{1,0:T(8,128)(2,1)} %all-gather.2.cloned.1.call-done, bf16[128,2048]{1,0:T(8,128)(2,1)} %bitcast.69), kind=kOutput, calls=%fused_computation.155 | convolution fusion | flops 1075314560 | bytes 12845568 | tf_op jit(solution)/shard_map/dot_general | solution.py:80
  164.7 4.5 all-to-all-start.1
  170.4 4.2 all-to-all-done.1
  174.7 8.6 %fusion.30 = (bf16[128,4096]{1,0:T(8,128)(2,1)S(1)}, bf16[128,4096]{1,0:T(8,128)(2,1)S(1)}, bf16[128,4096]{1,0:T(8,128)(2,1)S(1)}, bf16[128,4096]{1,0:T(8,128)(2...) fusion(f32[128,4096]{1,0:T(8,128)} %copy-done, ...), kind=kLoop, calls=%fused_computation.51 | loop fusion | flops 27787264 | bytes 27284480 | tf_op jit(solution)/shard_map/convert_element_type | solution.py:110
  190.0 1.8 convolution_dynamic-update-slice_fusion.3
  191.8 2.7 convolution_dynamic-update-slice_fusion.2
  194.5 4.5 convolution_dynamic-update-slice_fusion.1
  199.0 8.2 %convolution_dynamic-update-slice_fusion = f32[4096,2048]{0,1:T(8,128)} fusion(f32[4096,2048]{0,1:T(8,128)} %convolution_dynamic-update-slice_fusion.1, bf16[128,2048]{1,0:T(8,128)(2,1)S(1)} %bitcast.78, f32[128,4096]{1,0:T(8,128)S(1)} %copy-done.7, s32[4096]{0:T(1024)S(1)} %fusion.95, f32[128]{0:T(128)S(1)} %get-tuple-element.10, s32[128]{0:T(128)S(1)} %eq.17), kind=kOutput, calls=%fused_computation | convolution fusion | flops 1076887552 | bytes 19153920 | tf_op jit(solution)/shard_map/dot_general | solution.py:120
  207.2 33.3 %copy.33 = f32[4096,2048]{1,0:T(8,128)} copy(f32[4096,2048]{0,1:T(8,128)} %convolution_dynamic-update-slice_fusion) | data formatting | bytes 67108864 | tf_op jit(solution)/shard_map/concatenate | solution.py:130
  240.6 23.0 %copy.34 = f32[2,32,64,2048]{3,2,1,0:T(8,128)} copy(f32[2,32,64,2048]{3,2,0,1:T(8,128)} %bitcast.60) | data formatting | bytes 67108864 | tf_op jit(solution)/shard_map/transpose | solution.py:74
  263.9 41.7 %reduce-scatter.3.cloned.1.call-done = f32[32,64,2048]{2,1,0:T(8,128)} async-done(((f32[64,64,2048]{2,1,0:T(8,128)}), f32[32,64,2048]{2,1,0:T(8,128)}) %reduce-scatter.3.cloned.1.call-update) | async-done | bytes 16777232 | tf_op jit(solution)/shard_map/reduce_scatter | solution.py:75
  305.7 2.1 fusion.50
  307.8 1.8 fusion.47
  309.7 1.8 fusion.44
  313.4 2.4 fusion.38
  315.8 2.3 fusion.35
  318.1 2.4 fusion.31
  320.5 2.9 fusion.10
  323.4 4.9 fusion
  328.7 181.0 %all_to_all.21 = f32[2,64,2048]{2,1,0:T(8,128)S(1)} all-to-all(f32[2,64,2048]{2,1,0:T(8,128)S(1)} %bitcast.79), channel_id=1, replica_groups=mesh['dp_0'=4,'dp_1'=2,'dp_2'=4,'dp_3'=2,'rep'=2] {'rep'}, dimensions={0} | all-to-all | bytes 2097152 | tf_op jit(solution)/shard_map/all_to_all | solution.py:66
  510.5 4.3 reduce-scatter.5.cloned.1.call-done
  (97 shorter events, 22.5 us)
Async XLA Ops:
  7.2 17.3 %copy-start.30 = (s32[64]{0:T(128)S(1)}, s32[64]{0:T(128)}, u32[]{:S(2)}) copy-start(s32[64]{0:T(128)} %param.5) | copy-start | bytes 772
  7.2 126.6 %all-gather.2.cloned.1.call-start = ((), (), s32[]{:S(2)}) async-start(), calls=%async_computation.6 | async-start | bytes 17039360 | tf_op jit(solution)/shard_map/all_gather | solution.py:148
  9.7 14.7 %all-to-all-start = ((bf16[2,64,2048]{2,1,0:T(8,128)(2,1)}), bf16[2,64,2048]{2,1,0:T(8,128)(2,1)S(1)}, u32[]{:S(2)}, u32[]{:S(2)}) async-start(bf16[2,64,2048]{2,1,0:T(8,128)(2,1)} %broadcast_in_dim.10), calls=%async_computation | async-start | bytes 1048576 | tf_op jit(solution)/shard_map/all_to_all | solution.py:21
  24.4 111.5 %copy-start.11 = (bf16[2,64,2048]{2,1,0:T(8,128)(2,1)}, bf16[2,64,2048]{2,1,0:T(8,128)(2,1)S(1)}, u32[]{:S(2)}) copy-start(bf16[2,64,2048]{2,1,0:T(8,128)(2,1)S(1)} %all-to-all-done) | copy-start | bytes 1572868
  25.0 139.1 %all-to-all-start.2 = ((s32[2,1,64]{2,1,0:T(1,128)}), s32[2,1,64]{2,1,0:T(1,128)S(1)}, u32[]{:S(2)}, u32[]{:S(2)}) async-start(s32[2,1,64]{2,1,0:T(1,128)} %broadcast_in_dim.12), calls=%async_computation.2 | async-start | bytes 2048 | tf_op jit(solution)/shard_map/all_to_all | solution.py:21
  135.5 2.6 copy-start
  140.7 2.6 copy-start.2
  143.4 2.6 copy-start.3
  151.5 4.6 copy-start.5
  156.1 6.2 %copy-start.8 = (f32[128,4096]{1,0:T(8,128)}, f32[128,4096]{1,0:T(8,128)S(1)}, u32[]{:S(2)}) copy-start(f32[128,4096]{1,0:T(8,128)S(1)} %get-tuple-element.34) | copy-start | bytes 6291460
  164.7 9.9 %all-to-all-start.1 = ((f32[2,18,128]{2,1,0:T(8,128)}), f32[2,18,128]{2,1,0:T(8,128)S(1)}, u32[]{:S(2)}, u32[]{:S(2)}) async-start(f32[2,18,128]{2,1,0:T(8,128)} %broadcast_in_dim.11), calls=%async_computation.1 | async-start | bytes 49152 | tf_op jit(solution)/shard_map/all_to_all | solution.py:21
  169.2 136.4 %reduce-scatter.3.cloned.1.call-start = ((), (), s32[]{:S(2)}) async-start(), calls=%async_computation.7 | async-start | bytes 50331648 | tf_op jit(solution)/shard_map/reduce_scatter | solution.py:75
  170.4 28.6 %copy-start.28 = (s32[128]{0:T(128)}, s32[128]{0:T(128)S(1)}, u32[]{:S(2)}) copy-start(s32[128]{0:T(128)S(1)} %eq.17) | copy-start | bytes 1540
  174.7 24.3 %copy-start.26 = (f32[128]{0:T(128)}, f32[128]{0:T(128)S(1)}, u32[]{:S(2)}) copy-start(f32[128]{0:T(128)S(1)} %get-tuple-element.10) | copy-start | bytes 1540
  174.7 8.7 %copy-start.12 = (bf16[2,64,2048]{2,1,0:T(8,128)(2,1)S(1)}, bf16[2,64,2048]{2,1,0:T(8,128)(2,1)}, u32[]{:S(2)}) copy-start(bf16[2,64,2048]{2,1,0:T(8,128)(2,1)} %copy-done.11) | copy-start | bytes 1572868
  183.3 5.2 copy-start.17
  183.3 5.2 copy-start.19
  183.4 5.2 copy-start.15
  183.4 6.6 %copy-start.13 = (bf16[128,4096]{1,0:T(8,128)(2,1)}, bf16[128,4096]{1,0:T(8,128)(2,1)S(1)}, u32[]{:S(2)}) copy-start(bf16[128,4096]{1,0:T(8,128)(2,1)S(1)} %get-tuple-element.7) | copy-start | bytes 3145732
  183.4 11.1 %copy-start.21 = (bf16[128,4096]{1,0:T(8,128)(2,1)}, bf16[128,4096]{1,0:T(8,128)(2,1)S(1)}, u32[]{:S(2)}) copy-start(bf16[128,4096]{1,0:T(8,128)(2,1)S(1)} %get-tuple-element.3) | copy-start | bytes 3145732
  183.4 11.1 %copy-start.23 = (bf16[128,4096]{1,0:T(8,128)(2,1)}, bf16[128,4096]{1,0:T(8,128)(2,1)S(1)}, u32[]{:S(2)}) copy-start(bf16[128,4096]{1,0:T(8,128)(2,1)S(1)} %get-tuple-element.2) | copy-start | bytes 3145732
  183.4 11.1 %copy-start.9 = (bf16[128,4096]{1,0:T(8,128)(2,1)}, bf16[128,4096]{1,0:T(8,128)(2,1)S(1)}, u32[]{:S(2)}) copy-start(bf16[128,4096]{1,0:T(8,128)(2,1)S(1)} %get-tuple-element.9) | copy-start | bytes 3145732
  194.5 4.5 copy-start.7
  263.6 251.2 %reduce-scatter.5.cloned.1.call-start = ((), (), s32[]{:S(2)}) async-start(), calls=%async_computation.8 | async-start | bytes 17301504 | tf_op jit(solution)/shard_map/reduce_scatter | solution.py:76
  305.6 4.0 copy-start.20
  307.8 3.7 copy-start.18
  309.6 3.7 copy-start.16
  311.5 4.3 copy-start.14
  320.4 2.9 copy-start.27
  320.4 2.9 copy-start.29
  323.4 4.9 copy-start.24
  323.4 4.9 copy-start.25
  (5 other events, 11.0 us)
Sparse Core Ops, SparseCore 0:
  9.7 123.9 all-gather.1
  263.7 41.8 reduce-scatter.2
  308.6 206.1 reduce-scatter.4
where the time goes:
time: 523 us; the launch traced here: 521 us
  blocking collectives  181 us (35%)
  waiting for transfers between devices  166 us (32%)
  matrix products  70.7 us (14%)
  local copies, waits for them, and re-layouts  61.9 us (12%)
  other arithmetic  14.5 us (3%)
  between operations  14.2 us (3%)
  starting transfers between devices  13.2 us (3%)
    all_to_all x1, blocking collectives, sum_at_owner(): lax.all_to_all(blocks, axis, split_axis=0, concat_axis=0, tiled=True)  181 us
    all_gather x1, waiting for transfers between devices, on_device(): partner_docs = lax.all_gather(documents, DP, axis=0, tiled=True)  105 us
    reduce_scatter x1, waiting for transfers between devices, sum_by_chip(): blocks = lax.psum_scatter(blocks, core, scatter_dimension=0, tiled=True)  41.7 us
    concatenate x2, local copies, waits for them, and re-layouts, spread(): return jnp.concatenate(pieces, axis=1)  33.7 us
    dot_general x9, matrix products, contract(): lax.dot_general(first_op, second_op, (((1,), (1,)), ((), ())), preferred_...  24.4 us
    dot_general x9, matrix products, spread(): lax.dot_general(bands[nested], block_part, (((0,), (0,)), ((), ())), pref...  23.8 us
    transpose x1, local copies, waits for them, and re-layouts, sum_by_chip(): blocks = blocks.reshape(*sizes, *inside).swapaxes(0, 1).reshape(-1, *inside)  23 us
    dot_general x9, matrix products, spread(): jnp.dot(bands[nested], block_part, preferred_element_type=jnp.float32)  22.4 us
  transfers between devices with their start and end apart: 6, of which 5 were waited for; matrix products, arithmetic and copies ran while one was open for 11% of the time, Pallas kernels for 0%

commit v1 on v0

--- a/solution.py
+++ b/solution.py
@@ -145,7 +145,9 @@
     rep_index = lax.axis_index("rep")
     rep_count = lax.axis_size("rep")
     pair_rows, pair_partner = (collect(queries, "rep", 0), collect(partner, "rep", 0))
-    partner_docs = lax.all_gather(documents, DP, axis=0, tiled=True)
+    partner_docs = jnp.concatenate(
+        lax.all_to_all(jnp.stack([documents] * lax.axis_size(DP)), DP, 0, 0), axis=0
+    )
     col_pos = jnp.arange(partner_docs.shape[0], dtype=jnp.int32)
     col_ids = (col_pos // own_rows * rep_count + rep_index) * own_rows + col_pos % own_rows
     target = (pair_partner[:, None] == col_ids[None, :]).astype(jnp.float32)

time: 523 us -> 661 us (1.26)
  waiting for transfers between devices: 166 us -> 280 us
  blocking collectives: 181 us -> 196 us
    all_to_all x0 -> x1, waiting for transfers between devices: none -> 218 us  [on_device(): lax.all_to_all(jnp.stack([documents] * lax.axis_size(DP)), DP, 0, 0)]
    all_gather x1 -> x0, waiting for transfers between devices: 105 us -> none  [on_device(): partner_docs = lax.all_gather(documents, DP, axis=0, tiled=True)]
    all_to_all x0 -> x1, blocking collectives: none -> 14.5 us  [copy_for_each(): return lax.all_to_all(copies, axis, split_axis=0, concat_axis=0, tiled=True)]
    reduce_scatter x1, waiting for transfers between devices: 41.7 us -> 52.8 us  [sum_by_chip(): blocks = lax.psum_scatter(blocks, core, scatter_dimension=0, tiled=True)]
    all_to_all x3 -> x2, waiting for transfers between devices: 13.7 us -> 4.22 us  [copy_for_each(): return lax.all_to_all(copies, axis, split_axis=0, concat_axis=0, tiled=True)]
    all_to_all x0 -> x1, starting transfers between devices: none -> 8.79 us  [on_device(): lax.all_to_all(jnp.stack([documents] * lax.axis_size(DP)), DP, 0, 0)]
    another operation x0 -> x1, local copies, waits for them, and re-layouts: none -> 6.68 us  [on_device(): jnp.stack([documents] * lax.axis_size(DP))]
  transfers between devices with their start and end apart: 6 -> 5, of which waited for: 5 -> 4; matrix products, arithmetic and copies ran while one was open for 11% -> 8% of each run, Pallas kernels for 0% -> 0%
where the time goes in v1:
time: 661 us; the launch traced here: 660 us
  waiting for transfers between devices  280 us (42%)
  blocking collectives  196 us (30%)
  matrix products  71.2 us (11%)
  local copies, waits for them, and re-layouts  66.8 us (10%)
  starting transfers between devices  17 us (3%)
  other arithmetic  14.5 us (2%)
  between operations  14.5 us (2%)
    all_to_all x1, waiting for transfers between devices, on_device(): lax.all_to_all(jnp.stack([documents] * lax.axis_size(DP)), DP, 0, 0)  218 us
    all_to_all x1, blocking collectives, sum_at_owner(): lax.all_to_all(blocks, axis, split_axis=0, concat_axis=0, tiled=True)  181 us
    reduce_scatter x1, waiting for transfers between devices, sum_by_chip(): blocks = lax.psum_scatter(blocks, core, scatter_dimension=0, tiled=True)  52.8 us
    concatenate x2, local copies, waits for them, and re-layouts, spread(): return jnp.concatenate(pieces, axis=1)  33.7 us
    dot_general x9, matrix products, contract(): lax.dot_general(first_op, second_op, (((1,), (1,)), ((), ())), preferred_...  24.9 us
    dot_general x9, matrix products, spread(): lax.dot_general(bands[nested], block_part, (((0,), (0,)), ((), ())), pref...  23.8 us
    transpose x1, local copies, waits for them, and re-layouts, sum_by_chip(): blocks = blocks.reshape(*sizes, *inside).swapaxes(0, 1).reshape(-1, *inside)  23 us
    dot_general x9, matrix products, spread(): jnp.dot(bands[nested], block_part, preferred_element_type=jnp.float32)  22.4 us
  transfers between devices with their start and end apart: 5, of which 4 were waited for; matrix products, arithmetic and copies ran while one was open for 8% of the time, Pallas kernels for 0%

profile of v1, /device:TPU:0, one launch (start us, length us, event | category | flops | bytes accessed | tf_op | source)
XLA Modules:
  0.0 659.7 jit_solution(3719807217325395127)
XLA Ops:
  8.2 14.5 %all_to_all.26 = bf16[2,64,2048]{2,1,0:T(8,128)(2,1)S(1)} all-to-all(bf16[2,64,2048]{2,1,0:T(8,128)(2,1)S(1)} %broadcast_in_dim.10), channel_id=1, replica_groups=mesh['dp_0'=4,'dp_1'=2,'dp_2'=4,'dp_3'=2,'rep'=2] {'rep'}, dimensions={0} | all-to-all | bytes 1048576 | tf_op jit(solution)/shard_map/all_to_all | solution.py:21
  22.7 6.7 %stack.38 = bf16[64,64,2048]{2,1,0:T(8,128)(2,1)} broadcast(bf16[64,2048]{1,0:T(8,128)(2,1)} %param.4), dimensions={1,2} | broadcast | bytes 17039360 | tf_op jit(solution)/shard_map/stack | solution.py:149
  29.4 8.8 %all-to-all-start.1 = ((bf16[64,64,2048]{2,1,0:T(8,128)(2,1)}), bf16[64,64,2048]{2,1,0:T(8,128)(2,1)}, u32[]{:S(2)}, u32[]{:S(2)}) async-start(bf16[64,64,2048]{2,1,0:T(8,128)(2,1)} %stack.38), calls=%async_computation.1 | async-start | bytes 33554432 | tf_op jit(solution)/shard_map/all_to_all | solution.py:149
  38.2 218.2 %all-to-all-done.1 = bf16[64,64,2048]{2,1,0:T(8,128)(2,1)} async-done(((bf16[64,64,2048]{2,1,0:T(8,128)(2,1)}), bf16[64,64,2048]{2,1,0:T(8,128)(2,1)}, u32[]{:S(2)}, u32[]{:S(2)}) %all-to-all-start.1) | async-done | bytes 16777248 | tf_op jit(solution)/shard_map/all_to_all | solution.py:149
  256.9 3.2 all-to-all-start.3
  261.9 2.6 multiply_reduce_fusion.6
  265.0 2.1 multiply_reduce_fusion.5
  267.6 2.1 multiply_reduce_fusion.4
  270.3 2.1 multiply_reduce_fusion.3
  272.9 2.0 multiply_reduce_fusion.2
  275.4 2.5 multiply_reduce_fusion.1
  278.4 4.1 multiply_reduce_fusion
  283.0 5.7 fusion.110
  290.7 4.8 all-to-all-start.2
  296.7 4.2 all-to-all-done.2
  300.9 8.6 %fusion.30 = (bf16[128,4096]{1,0:T(8,128)(2,1)S(1)}, bf16[128,4096]{1,0:T(8,128)(2,1)S(1)}, bf16[128,4096]{1,0:T(8,128)(2,1)S(1)}, bf16[128,4096]{1,0:T(8,128)(2...) fusion(f32[128,4096]{1,0:T(8,128)} %copy-done, ...), kind=kLoop, calls=%fused_computation.51 | loop fusion | flops 27787264 | bytes 27284480 | tf_op jit(solution)/shard_map/convert_element_type | solution.py:110
  316.2 1.8 convolution_dynamic-update-slice_fusion.3
  318.0 2.7 convolution_dynamic-update-slice_fusion.2
  320.7 4.5 convolution_dynamic-update-slice_fusion.1
  325.2 8.2 %convolution_dynamic-update-slice_fusion = f32[4096,2048]{0,1:T(8,128)} fusion(f32[4096,2048]{0,1:T(8,128)} %convolution_dynamic-update-slice_fusion.1, bf16[128,2048]{1,0:T(8,128)(2,1)S(1)} %bitcast.79, f32[128,4096]{1,0:T(8,128)S(1)} %copy-done.7, s32[4096]{0:T(1024)S(1)} %fusion.95, f32[128]{0:T(128)S(1)} %get-tuple-element.10, s32[128]{0:T(128)S(1)} %eq.17), kind=kOutput, calls=%fused_computation | convolution fusion | flops 1076887552 | bytes 19153920 | tf_op jit(solution)/shard_map/dot_general | solution.py:120
  333.5 33.3 %copy.33 = f32[4096,2048]{1,0:T(8,128)} copy(f32[4096,2048]{0,1:T(8,128)} %convolution_dynamic-update-slice_fusion) | data formatting | bytes 67108864 | tf_op jit(solution)/shard_map/concatenate | solution.py:130
  366.8 23.0 %copy.34 = f32[2,32,64,2048]{3,2,1,0:T(8,128)} copy(f32[2,32,64,2048]{3,2,0,1:T(8,128)} %bitcast.61) | data formatting | bytes 67108864 | tf_op jit(solution)/shard_map/transpose | solution.py:74
  390.1 52.8 %reduce-scatter.3.cloned.1.call-done = f32[32,64,2048]{2,1,0:T(8,128)} async-done(((f32[64,64,2048]{2,1,0:T(8,128)}), f32[32,64,2048]{2,1,0:T(8,128)}) %reduce-scatter.3.cloned.1.call-update) | async-done | bytes 16777232 | tf_op jit(solution)/shard_map/reduce_scatter | solution.py:75
  443.0 2.1 fusion.50
  447.0 1.8 fusion.44
  450.7 2.4 fusion.38
  453.1 2.3 fusion.35
  455.4 2.4 fusion.31
  457.8 2.9 fusion.10
  460.7 4.9 fusion
  466.0 181.0 %all_to_all.27 = f32[2,64,2048]{2,1,0:T(8,128)S(1)} all-to-all(f32[2,64,2048]{2,1,0:T(8,128)S(1)} %bitcast.80), channel_id=1, replica_groups=mesh['dp_0'=4,'dp_1'=2,'dp_2'=4,'dp_3'=2,'rep'=2] {'rep'}, dimensions={0} | all-to-all | bytes 2097152 | tf_op jit(solution)/shard_map/all_to_all | solution.py:66
  647.9 5.0 reduce-scatter.5.cloned.1.call-done
  (96 shorter events, 21.9 us)
Async XLA Ops:
  22.7 239.2 %copy-start.11 = (bf16[2,64,2048]{2,1,0:T(8,128)(2,1)}, bf16[2,64,2048]{2,1,0:T(8,128)(2,1)S(1)}, u32[]{:S(2)}) copy-start(bf16[2,64,2048]{2,1,0:T(8,128)(2,1)S(1)} %all_to_all.26) | copy-start | bytes 1572868
  29.4 227.0 %copy-start.30 = (s32[64]{0:T(128)S(1)}, s32[64]{0:T(128)}, u32[]{:S(2)}) copy-start(s32[64]{0:T(128)} %param.5) | copy-start | bytes 772
  29.4 227.0 %all-to-all-start.1 = ((bf16[64,64,2048]{2,1,0:T(8,128)(2,1)}), bf16[64,64,2048]{2,1,0:T(8,128)(2,1)}, u32[]{:S(2)}, u32[]{:S(2)}) async-start(bf16[64,64,2048]{2,1,0:T(8,128)(2,1)} %stack.38), calls=%async_computation.1 | async-start | bytes 33554432 | tf_op jit(solution)/shard_map/all_to_all | solution.py:149
  256.9 33.2 %all-to-all-start.3 = ((s32[2,1,64]{2,1,0:T(1,128)}), s32[2,1,64]{2,1,0:T(1,128)S(1)}, u32[]{:S(2)}, u32[]{:S(2)}) async-start(s32[2,1,64]{2,1,0:T(1,128)} %broadcast_in_dim.12), calls=%async_computation.3 | async-start | bytes 2048 | tf_op jit(solution)/shard_map/all_to_all | solution.py:21
  261.9 2.7 copy-start
  264.5 2.6 copy-start.1
  267.1 2.6 copy-start.2
  269.7 2.6 copy-start.3
  277.9 4.6 copy-start.5
  282.5 6.2 copy-start.8
  290.7 10.2 %all-to-all-start.2 = ((f32[2,18,128]{2,1,0:T(8,128)}), f32[2,18,128]{2,1,0:T(8,128)S(1)}, u32[]{:S(2)}, u32[]{:S(2)}) async-start(f32[2,18,128]{2,1,0:T(8,128)} %broadcast_in_dim.11), calls=%async_computation.2 | async-start | bytes 49152 | tf_op jit(solution)/shard_map/all_to_all | solution.py:21
  295.5 147.5 %reduce-scatter.3.cloned.1.call-start = ((), (), s32[]{:S(2)}) async-start(), calls=%async_computation.7 | async-start | bytes 50331648 | tf_op jit(solution)/shard_map/reduce_scatter | solution.py:75
  296.7 28.6 %copy-start.28 = (s32[128]{0:T(128)}, s32[128]{0:T(128)S(1)}, u32[]{:S(2)}) copy-start(s32[128]{0:T(128)S(1)} %eq.17) | copy-start | bytes 1540
  300.9 24.3 %copy-start.26 = (f32[128]{0:T(128)}, f32[128]{0:T(128)S(1)}, u32[]{:S(2)}) copy-start(f32[128]{0:T(128)S(1)} %get-tuple-element.10) | copy-start | bytes 1540
  300.9 8.7 %copy-start.12 = (bf16[2,64,2048]{2,1,0:T(8,128)(2,1)S(1)}, bf16[2,64,2048]{2,1,0:T(8,128)(2,1)}, u32[]{:S(2)}) copy-start(bf16[2,64,2048]{2,1,0:T(8,128)(2,1)} %copy-done.11) | copy-start | bytes 1572868
  309.6 5.2 copy-start.17
  309.6 5.2 copy-start.19
  309.6 5.2 copy-start.15
  309.6 6.6 %copy-start.13 = (bf16[128,4096]{1,0:T(8,128)(2,1)}, bf16[128,4096]{1,0:T(8,128)(2,1)S(1)}, u32[]{:S(2)}) copy-start(bf16[128,4096]{1,0:T(8,128)(2,1)S(1)} %get-tuple-element.7) | copy-start | bytes 3145732
  309.6 11.1 %copy-start.21 = (bf16[128,4096]{1,0:T(8,128)(2,1)}, bf16[128,4096]{1,0:T(8,128)(2,1)S(1)}, u32[]{:S(2)}) copy-start(bf16[128,4096]{1,0:T(8,128)(2,1)S(1)} %get-tuple-element.3) | copy-start | bytes 3145732
  309.6 11.1 %copy-start.23 = (bf16[128,4096]{1,0:T(8,128)(2,1)}, bf16[128,4096]{1,0:T(8,128)(2,1)S(1)}, u32[]{:S(2)}) copy-start(bf16[128,4096]{1,0:T(8,128)(2,1)S(1)} %get-tuple-element.2) | copy-start | bytes 3145732
  309.6 11.1 %copy-start.9 = (bf16[128,4096]{1,0:T(8,128)(2,1)}, bf16[128,4096]{1,0:T(8,128)(2,1)S(1)}, u32[]{:S(2)}) copy-start(bf16[128,4096]{1,0:T(8,128)(2,1)S(1)} %get-tuple-element.9) | copy-start | bytes 3145732
  320.7 4.5 copy-start.7
  389.8 263.0 %reduce-scatter.5.cloned.1.call-start = ((), (), s32[]{:S(2)}) async-start(), calls=%async_computation.8 | async-start | bytes 17301504 | tf_op jit(solution)/shard_map/reduce_scatter | solution.py:76
  443.0 4.0 copy-start.20
  445.1 3.7 copy-start.18
  447.0 3.7 copy-start.16
  448.9 4.3 copy-start.14
  457.8 2.9 copy-start.27
  457.8 2.9 copy-start.29
  460.7 4.9 copy-start.24
  460.7 4.9 copy-start.25
  (4 other events, 8.4 us)
Sparse Core Ops, SparseCore 0:
  390.0 52.9 reduce-scatter.2
  445.9 206.8 reduce-scatter.4
